TPU v7x, 128 devices: a whole 4x4x4 slice. The times are simulated.
128 devices in a mesh: dp: 4 (over z), seq: 32 (over x, y, core).
Axes of the slice: x: 4, y: 4, z: 4, core: 2. Of those that a mesh axis runs over, the one named last changes fastest.
Arguments:
- queries: bfloat16 [4, 4096, 4096], P('dp', 'seq'), may hold values from -6 to 6
- keys: bfloat16 [4, 4096, 4096], P('dp', 'seq'), may hold values from -6 to 6
- values: bfloat16 [4, 4096, 4096], P('dp', 'seq'), may hold values from -6 to 6
- log_decay: float32 [4, 32, 4096], P('dp', None, 'seq'), may hold values from -1 to 0
- attn_grad: bfloat16 [4, 4096, 4096], P('dp', 'seq'), may hold values from -6 to 6
- norm_gain: float32 [4096], replicated, may hold values from 0.1 to 1.9
- route_ids: int32 [4, 4096, 2], P('dp', 'seq'), may hold values from 0 to 31, all different within a row; in each aligned block of 128 rows (0 to 127, 128 to 255, ..., all dimensions but the last counted through in order) at most 10 rows name the same one
- route_weights: float32 [4, 4096, 2], P('dp', 'seq'), may hold values from 0.2 to 1
- grad_exponent: int32 [32], replicated, may hold values from -2 to 2
- w_in: bfloat16 [32, 4608, 4096], P('seq', 'dp'), may hold values from -0.09375 to 0.09375
- w_out: bfloat16 [32, 4608, 4096], P('seq', 'dp'), may hold values from -0.09375 to 0.09375
Outputs:
- layer_out: bfloat16 [4, 4096, 4096], P('dp', 'seq')
- key_out: bfloat16 [4, 4096, 4096], P('dp', 'seq')
- value_out: bfloat16 [4, 4096, 4096], P('dp', 'seq')
Inputs may be any that keep to these rules, and one draw needn't show every extreme that they name: `route_ids`: in each aligned block of 128 tokens (the tokens of one device) no expert is chosen by more than 10 tokens, a bound that some block reaches; a token's 2 choices differ.
All inputs are finite; a program needn't handle non-finite values.
Results may differ from a plain program's by a relative error of at most 0.019.
Values may be sent and summed in bfloat16 or wider, within the bound.
A program may use at most 320 MiB of HBM per device.

v0:
```python
import jax
import jax.numpy as jnp
from jax import lax
from jax.sharding import Mesh
from jax.sharding import PartitionSpec as P

ATTENTION_HEADS = 32
HEAD = 128
TOP = 2
SEQ = ("seq_0", "seq_1", "seq_2")


norm_eps = 1e-06
highest = lax.Precision.HIGHEST


def prefix(shard, axis, join, neutral):
    place = lax.axis_index(axis)
    gathered = jax.tree.map(
        lambda a, kind: lax.all_gather(a.astype(kind), axis), shard, (jnp.bfloat16, jnp.bfloat16)
    )
    state = jax.tree.map(lambda a, e: jnp.zeros_like(a) + jnp.asarray(e, a.dtype), shard, neutral)

    def one(lap, state):
        return join(
            state,
            jax.tree.map(
                lambda a, own: lax.dynamic_index_in_dim(a, lap, 0, False).astype(own.dtype),
                gathered,
                shard,
            ),
        )

    return lax.fori_loop(0, place, one, state)


def filled_with(shard, identity):
    return jax.tree.map(
        lambda part, zero: jnp.zeros_like(part) + jnp.asarray(zero, part.dtype), shard, identity
    )


def entering(shard, axes, combine, identity):
    before = start = filled_with(shard, identity)
    running = shard
    for axis in reversed(axes):
        length, position = (lax.axis_size(axis), lax.axis_index(axis))
        pieces = jax.tree.map(
            lambda part, kind: lax.all_gather(part.astype(kind), axis),
            running,
            (jnp.bfloat16, jnp.bfloat16),
        )
        inside, running = (start, start)
        for k in reversed(range(length)):
            passed = k > position
            running = combine(
                running, jax.tree.map(lambda part, own: part[k].astype(own.dtype), pieces, shard)
            )
            inside = jax.tree.map(lambda new, old: jnp.where(passed, new, old), running, inside)
        before = combine(inside, before)
    return before


def combine_states(earlier, following):
    return (earlier[0] * following[0], following[0][:, None, None] * earlier[1] + following[1])


def expert_slice(row_block, weight_in, weight_out):
    hidden = jax.nn.silu(
        lax.dot_general(
            row_block, weight_in, (((1,), (1,)), ((), ())), preferred_element_type=jnp.float32
        )
    ).astype(jnp.bfloat16)
    return jnp.dot(hidden, weight_out, preferred_element_type=jnp.float32)


def on_device(
    queries,
    keys,
    values,
    log_decay,
    attn_grad,
    norm_gain,
    route_ids,
    route_weights,
    grad_exponent,
    w_in,
    w_out,
):
    length = queries.shape[1]
    width = queries.shape[2]
    query_heads = queries[0].reshape(length, ATTENTION_HEADS, HEAD)
    key_heads = keys[0].reshape(length, ATTENTION_HEADS, HEAD)
    value_heads = values[0].reshape(length, ATTENTION_HEADS, HEAD)
    grad_heads = attn_grad[0].reshape(length, ATTENTION_HEADS, HEAD)
    running = jnp.cumsum(log_decay[0], axis=1)
    block_total = running[:, -1]
    position_indices = jnp.arange(length)
    lower_mask = position_indices[:, None] >= position_indices[None, :]
    spread = running[:, :, None] - running[:, None, :]
    weight = jnp.where(lower_mask, jnp.exp(jnp.where(lower_mask, spread, 0.0)), 0.0)
    head_major = running.T
    tail_decay = jnp.exp(block_total[None, :] - head_major)[..., None]
    lead_decay = jnp.exp(head_major)[..., None]
    score_scale = 1.0 / HEAD
    query_wide = query_heads.astype(jnp.float32)
    key_wide = key_heads.astype(jnp.float32)
    value_wide = value_heads.astype(jnp.float32)
    local_state = jnp.einsum("shp,shq->hpq", key_wide * tail_decay, value_wide, precision=highest)
    back_local = jnp.einsum(
        "thp,thq->hpq", query_wide * lead_decay, grad_heads.astype(jnp.float32), precision=highest
    )
    decay_total = jnp.exp(block_total)
    identity = (
        jnp.ones((ATTENTION_HEADS,), jnp.float32),
        jnp.zeros((ATTENTION_HEADS, HEAD, HEAD), jnp.float32),
    )
    state_in = prefix((decay_total, local_state), SEQ, combine_states, identity)[1]
    back_in = entering((decay_total, back_local), SEQ, combine_states, identity)[1]
    scores = jnp.einsum("thp,shp->hts", query_heads, key_heads, preferred_element_type=jnp.float32)
    attn_probs = (scores * weight * score_scale).astype(jnp.bfloat16)
    grad_probs = (
        jnp.einsum("thq,shq->hts", grad_heads, value_heads, preferred_element_type=jnp.float32)
        * weight
        * score_scale
    ).astype(jnp.bfloat16)
    attention = jnp.einsum(
        "hts,shp->thp", attn_probs, value_heads, preferred_element_type=jnp.float32
    )
    attention = attention + score_scale * lead_decay * jnp.einsum(
        "thp,hpq->thq", query_wide, state_in, precision=highest
    )
    attn_out = attention.reshape(length, width).astype(jnp.bfloat16)
    factor = jnp.exp2(grad_exponent.astype(jnp.float32))[None, :, None]
    key_grad = jnp.einsum(
        "hts,thp->shp", grad_probs, query_heads, preferred_element_type=jnp.float32
    )
    key_grad = key_grad + score_scale * tail_decay * jnp.einsum(
        "shq,hpq->shp", value_wide, back_in, precision=highest
    )
    value_grad = jnp.einsum(
        "hts,thq->shq", attn_probs, grad_heads, preferred_element_type=jnp.float32
    )
    value_grad = value_grad + score_scale * tail_decay * jnp.einsum(
        "shp,hpq->shq", key_wide, back_in, precision=highest
    )
    key_out = (key_grad * factor).reshape(1, length, width).astype(jnp.bfloat16)
    value_out = (value_grad * factor).reshape(1, length, width).astype(jnp.bfloat16)
    attn_wide = attn_out.astype(jnp.float32)
    mean_square = jnp.mean(attn_wide * attn_wide, axis=-1, keepdims=True)
    normed = (attn_wide * lax.rsqrt(mean_square + norm_eps) * norm_gain).astype(jnp.bfloat16)
    experts_total = w_in.shape[0] * lax.axis_size(SEQ)
    capacity = max(2, TOP * length * 5 // (4 * experts_total))
    choice_ids = route_ids[0].reshape(length * TOP)
    onehot = (choice_ids[:, None] == jnp.arange(experts_total, dtype=jnp.int32)[None, :]).astype(
        jnp.int32
    )
    slot_index = jnp.sum((jnp.cumsum(onehot, axis=0) - 1) * onehot, axis=-1)
    target = choice_ids * capacity + slot_index
    send_buffer = (
        jnp.zeros((experts_total * capacity, width), jnp.bfloat16)
        .at[target]
        .set(jnp.repeat(normed, TOP, axis=0))
    )
    arrived = lax.all_to_all(
        send_buffer.reshape(experts_total, capacity, width),
        SEQ,
        split_axis=0,
        concat_axis=0,
        tiled=True,
    )
    weight_in = w_in[0]
    weight_out = w_out[0]
    pooled = lax.all_gather(arrived, "dp", axis=0, tiled=True).reshape(-1, width)
    summed = lax.psum_scatter(
        expert_slice(pooled, weight_in, weight_out).astype(jnp.bfloat16),
        "dp",
        scatter_dimension=0,
        tiled=True,
    )
    expert_out = summed.reshape(experts_total, capacity, width)
    returned = lax.all_to_all(expert_out, SEQ, split_axis=0, concat_axis=0, tiled=True).reshape(
        experts_total * capacity, width
    )
    picked = returned[target].reshape(length, TOP, width)
    mixed_rows = attn_wide + jnp.sum(
        route_weights[0][..., None] * picked.astype(jnp.float32), axis=1
    )
    layer_out = mixed_rows.astype(jnp.bfloat16).reshape(1, length, width)
    return (layer_out, key_out, value_out)


def solution(mesh):
    split = Mesh(mesh.devices.reshape(mesh.shape["dp"], 4, 4, 2), ("dp", "seq_0", "seq_1", "seq_2"))
    placed = (
        P("dp", SEQ, None),
        P("dp", SEQ, None),
        P("dp", SEQ, None),
        P("dp", None, SEQ),
        P("dp", SEQ, None),
        P(),
        P("dp", SEQ, None),
        P("dp", SEQ, None),
        P(),
        P(SEQ, "dp", None),
        P(SEQ, "dp", None),
    )
    return jax.shard_map(
        on_device,
        mesh=split,
        in_specs=placed,
        out_specs=(P("dp", SEQ, None), P("dp", SEQ, None), P("dp", SEQ, None)),
        check_vma=False,
    )
```

profile of v0, /device:TPU:1, one launch (start us, length us, event | category | flops | bytes accessed | tf_op | source)
XLA Modules:
  0.0 685.1 jit_solution(15141601596157490291)
XLA Ops:
  16.1 65.7 %all-reduce = bf16[1024]{0:T(1024)(128)(2,1)S(1)} all-reduce(bf16[1024]{0:T(1024)(128)(2,1)S(1)} %dynamic-update-slice), channel_id=2, replica_groups=mesh['dp'=4,'seq_0'=4,'seq_1'=4,'seq_2'=2] {'seq_0','seq_1','seq_2'}, use_global_device_ids=true, to_apply=%add | all-reduce | flops 1024 | bytes 4096
  91.5 40.3 %all-gather.18.cloned.1.call-done = bf16[1024,128,128]{2,1,0:T(8,128)(2,1)} async-done(((bf16[32,128,128]{2,1,0:T(8,128)(2,1)}), bf16[1024,128,128]{2,1,0:T(8,128)(2,1)}) %all-gather.18.cloned.1.call-update) | async-done | bytes 33554448 | tf_op jit(solution)/shard_map/all_gather | solution.py:20
  146.9 6.3 scatter_custom_fusion
  153.1 4.6 reshape.302
  157.8 55.8 %all-to-all-start = ((bf16[32,10,4096]{2,1,0:T(8,128)(2,1)}), bf16[32,10,4096]{2,1,0:T(8,128)(2,1)}, u32[]{:S(2)}, u32[]{:S(2)}) async-start(bf16[32,10,4096]{2,1,0:T(8,128)(2,1)} %reshape.302), calls=%async_computation | async-start | bytes 8388608 | tf_op jit(solution)/shard_map/all_to_all | solution.py:165
  217.0 48.7 %all-to-all-done = bf16[32,10,4096]{2,1,0:T(8,128)(2,1)} async-done(((bf16[32,10,4096]{2,1,0:T(8,128)(2,1)}), bf16[32,10,4096]{2,1,0:T(8,128)(2,1)}, u32[]{:S(2)}, u32[]{:S(2)}) %all-to-all-start) | async-done | bytes 2621472 | tf_op jit(solution)/shard_map/all_to_all | solution.py:165
  265.7 5.2 copy.69
  275.8 7.4 %all-gather.4 = bf16[4,1,32]{2,1,0:T(2,128)(2,1)S(1)} all-gather(bf16[1,1,32]{2,1,0:T(2,128)(2,1)S(1)} %convert_bitcast_fusion.6), channel_id=1, replica_groups=mesh['dp'=4,'seq_0'=4,'seq_1'=4,'seq_2'=2] {'seq_1'}, dimensions={0}, use_global_device_ids=true | all-gather | bytes 320 | tf_op jit(solution)/shard_map/all_gather | solution.py:49
  286.7 85.6 %all-gather.12.cloned.1.call-done = bf16[128,10,4096]{2,0,1:T(8,128)(2,1)} async-done(((bf16[32,10,4096]{2,0,1:T(8,128)(2,1)}), bf16[128,10,4096]{2,0,1:T(8,128)(2,1)}) %all-gather.12.cloned.1.call-update) | async-done | bytes 10485776 | tf_op jit(solution)/shard_map/all_gather | solution.py:174
  372.3 15.3 %copy.70 = bf16[128,10,4096]{2,1,0:T(8,128)(2,1)} copy(bf16[128,10,4096]{2,0,1:T(8,128)(2,1)} %all-gather.12.cloned.1.call-done) | data formatting | bytes 20971520 | tf_op jit(solution)/shard_map/all_gather | solution.py:174
  387.5 16.8 %reshape.303 = bf16[1280,4096]{1,0:T(8,128)(2,1)} reshape(bf16[128,10,4096]{2,1,0:T(8,128)(2,1)} %copy.70) | data formatting | bytes 20971520 | tf_op jit(solution)/shard_map/reshape | solution.py:174
  404.3 19.4 %multiply_convert_fusion = bf16[1280,1152]{1,0:T(8,128)(2,1)S(1)} fusion(bf16[1280,4096]{1,0:T(8,128)(2,1)} %reshape.303, bf16[1,1152,4096]{2,1,0:T(8,128)(2,1)} %param.22), kind=kOutput, calls=%fused_computation.8 | convolution fusion | flops 12086968320 | bytes 22872064 | tf_op jit(solution)/shard_map/dot_general | solution.py:70
  423.8 16.0 %convolution_convert_fusion = bf16[1280,4096]{1,0:T(8,128)(2,1)} fusion(bf16[1280,1152]{1,0:T(8,128)(2,1)S(1)} %multiply_convert_fusion, bf16[1,1152,4096]{2,1,0:T(8,128)(2,1)S(1)} %bitcast.271), kind=kOutput, calls=%fused_computation.4 | convolution fusion | flops 12084838400 | bytes 22872064 | tf_op jit(solution)/shard_map/dot_general | solution.py:74
  439.9 4.1 fusion.23
  444.1 7.6 %all-gather.5 = bf16[4,1,32]{2,1,0:T(2,128)(2,1)S(1)} all-gather(bf16[1,1,32]{2,1,0:T(2,128)(2,1)S(1)} %fusion.86), channel_id=1, replica_groups=mesh['dp'=4,'seq_0'=4,'seq_1'=4,'seq_2'=2] {'seq_0'}, dimensions={0}, use_global_device_ids=true | all-gather | bytes 320 | tf_op jit(solution)/shard_map/all_gather | solution.py:49
  451.8 86.9 %reduce-scatter.2.cloned.1.call-done = bf16[320,4096]{1,0:T(8,128)(2,1)} async-done(((bf16[1280,4096]{1,0:T(8,128)(2,1)}), bf16[320,4096]{1,0:T(8,128)(2,1)}) %reduce-scatter.2.cloned.1.call-update) | async-done | bytes 2621456 | tf_op jit(solution)/shard_map/reduce_scatter | solution.py:175
  538.7 4.6 reshape.304
  543.3 8.2 %all-to-all-start.1 = ((bf16[32,10,4096]{2,1,0:T(8,128)(2,1)}), bf16[32,10,4096]{2,1,0:T(8,128)(2,1)}, u32[]{:S(2)}, u32[]{:S(2)}) async-start(bf16[32,10,4096]{2,1,0:T(8,128)(2,1)} %reshape.304), calls=%async_computation.2 | async-start | bytes 8388608 | tf_op jit(solution)/shard_map/all_to_all | solution.py:182
  551.6 76.3 %all-gather.16.cloned.1.call-done = bf16[4,32,128,128]{3,2,1,0:T(8,128)(2,1)} async-done(((bf16[1,32,128,128]{3,2,1,0:T(8,128)(2,1)}), bf16[4,32,128,128]{3,2,1,0:T(8,128)(2,1)}) %all-gather.16.cloned.1.call-update) | async-done | bytes 4194320 | tf_op jit(solution)/shard_map/all_gather | solution.py:49
  627.9 8.4 %fusion.9 = f32[32,128,128]{2,1,0:T(8,128)S(1)} fusion(bf16[4,32,128,128]{3,2,1,0:T(8,128)(2,1)} %all-gather.16.cloned.1.call-done, f32[32]{0:T(128)S(1)} %get-tuple-element.79, f32[32]{0:T(128)S(1)} %slice_convert_fusion.5, f32[32]{0:T(128)S(1)} %get-tuple-element.75, f32[32]{0:T(128)S(1)} %get-tuple-element.77, f32[32]{0:T(128)S(1)} %get-tuple-element.78, ...), kind=kLoop, calls=%fused_computation.26 | loop fusion | flops 21495808 | bytes 12584458 | tf_op jit(solution)/shard_map/add | solution.py:65
  642.1 3.8 fusion.70
  645.9 4.8 fusion.40
  661.5 5.6 reshape.310
  667.2 8.9 %multiply_reduce_fusion = f32[128,4096]{1,0:T(8,128)S(1)} fusion(f32[128,2,4096]{2,1,0:T(2,128)} %reshape.310, f32[128,2]{1,0:T(8,128)S(1)} %copy.63), kind=kLoop, calls=%fused_computation.9 | loop fusion | flops 1572864 | bytes 6292480 | tf_op jit(solution)/shard_map/reduce_sum | solution.py:186
  (122 shorter events, 62.7 us)
Async XLA Ops:
  8.0 2.9 copy-start.11
  8.0 123.8 %all-gather.18.cloned.1.call-start = ((), (), s32[]{:S(2)}) async-start(), calls=%async_computation.7 | async-start | bytes 34603008 | tf_op jit(solution)/shard_map/all_gather | solution.py:20
  11.5 75.5 %copy-start.2 = (bf16[1,128,4096]{1,2,0:T(8,128)(2,1)}, bf16[1,128,4096]{1,2,0:T(8,128)(2,1)S(1)}, u32[]{:S(2)}) copy-start(bf16[1,128,4096]{1,2,0:T(8,128)(2,1)S(1)} %copy.86) | copy-start | bytes 3145732
  11.5 2.5 copy-start.13
  11.6 2.9 copy-start.17
  83.5 4.7 copy-start.6
  134.0 5.1 copy-start.12
  157.8 55.9 %copy-start.4 = (bf16[1,128,4096]{1,2,0:T(8,128)(2,1)S(1)}, bf16[1,128,4096]{1,2,0:T(8,128)(2,1)}, u32[]{:S(2)}) copy-start(bf16[1,128,4096]{1,2,0:T(8,128)(2,1)} %copy.87) | copy-start | bytes 3145732
  157.8 55.9 %copy-start.7 = (bf16[1,128,4096]{1,2,0:T(8,128)(2,1)S(1)}, bf16[1,128,4096]{1,2,0:T(8,128)(2,1)}, u32[]{:S(2)}) copy-start(bf16[1,128,4096]{1,2,0:T(8,128)(2,1)} %copy-done.6) | copy-start | bytes 3145732
  157.8 107.9 %all-to-all-start = ((bf16[32,10,4096]{2,1,0:T(8,128)(2,1)}), bf16[32,10,4096]{2,1,0:T(8,128)(2,1)}, u32[]{:S(2)}, u32[]{:S(2)}) async-start(bf16[32,10,4096]{2,1,0:T(8,128)(2,1)} %reshape.302), calls=%async_computation | async-start | bytes 8388608 | tf_op jit(solution)/shard_map/all_to_all | solution.py:165
  213.6 69.7 %all-gather.20.cloned.1.call-start = ((), (), s32[]{:S(2)}) async-start(), calls=%async_computation.8 | async-start | bytes 3145728 | tf_op jit(solution)/shard_map/all_gather | solution.py:49
  217.0 155.3 %all-gather.12.cloned.1.call-start = ((), (), s32[]{:S(2)}) async-start(), calls=%async_computation.3 | async-start | bytes 13107200 | tf_op jit(solution)/shard_map/all_gather | solution.py:174
  270.9 169.1 %all-gather.14.cloned.1.call-start = ((), (), s32[]{:S(2)}) async-start(), calls=%async_computation.5 | async-start | bytes 5242880 | tf_op jit(solution)/shard_map/all_gather | solution.py:49
  286.6 252.1 %reduce-scatter.2.cloned.1.call-start = ((), (), s32[]{:S(2)}) async-start(), calls=%async_computation.4 | async-start | bytes 13107200 | tf_op jit(solution)/shard_map/reduce_scatter | solution.py:175
  387.5 36.2 %slice-start = ((s8[9437184]{0:T(1024)(128)(4,1)}), s8[1048576]{0:T(1024)(128)(4,1)S(1)}, s32[]{:S(2)}) async-start(s8[9437184]{0:T(1024)(128)(4,1)} %bitcast.270), calls=%async_computation.9 | async-start | bytes 2097152
  404.3 19.4 %slice-start.1 = ((s8[9437184]{0:T(1024)(128)(4,1)}), s8[4194304]{0:T(1024)(128)(4,1)S(1)}, s32[]{:S(2)}) async-start(s8[9437184]{0:T(1024)(128)(4,1)} %bitcast.270), calls=%async_computation.10 | async-start | bytes 8388608
  404.3 19.5 %slice-start.2 = ((s8[9437184]{0:T(1024)(128)(4,1)}), s8[4194304]{0:T(1024)(128)(4,1)S(1)}, s32[]{:S(2)}) async-start(s8[9437184]{0:T(1024)(128)(4,1)} %bitcast.270), calls=%async_computation.11 | async-start | bytes 8388608
  439.8 188.1 %all-gather.16.cloned.1.call-start = ((), (), s32[]{:S(2)}) async-start(), calls=%async_computation.6 | async-start | bytes 5242880 | tf_op jit(solution)/shard_map/all_gather | solution.py:49
  543.3 8.2 %copy-start.15 = (s32[32]{0:T(128)S(1)}, s32[32]{0:T(128)}, u32[]{:S(2)}) copy-start(s32[32]{0:T(128)} %param.21) | copy-start | bytes 388
  543.3 8.2 %copy-start.14 = (f32[1,128,2]{1,2,0:T(2,128)S(1)}, f32[1,128,2]{1,2,0:T(2,128)}, u32[]{:S(2)}) copy-start(f32[1,128,2]{1,2,0:T(2,128)} %param.20) | copy-start | bytes 3076
  543.3 111.7 %all-to-all-start.1 = ((bf16[32,10,4096]{2,1,0:T(8,128)(2,1)}), bf16[32,10,4096]{2,1,0:T(8,128)(2,1)}, u32[]{:S(2)}, u32[]{:S(2)}) async-start(bf16[32,10,4096]{2,1,0:T(8,128)(2,1)} %reshape.304), calls=%async_computation.2 | async-start | bytes 8388608 | tf_op jit(solution)/shard_map/all_to_all | solution.py:182
  627.9 8.4 %copy-start.3 = (bf16[1,128,4096]{1,2,0:T(8,128)(2,1)S(1)}, bf16[1,128,4096]{1,2,0:T(8,128)(2,1)}, u32[]{:S(2)}) copy-start(bf16[1,128,4096]{1,2,0:T(8,128)(2,1)} %copy-done.2) | copy-start | bytes 3145732
  650.7 2.4 copy-start.1
  667.1 8.9 %copy-start.8 = (f32[1,128,4096]{2,1,0:T(8,128)S(1)}, f32[1,128,4096]{2,1,0:T(8,128)}, u32[]{:S(2)}) copy-start(f32[1,128,4096]{2,1,0:T(8,128)} %copy.71) | copy-start | bytes 6291460
  (5 other events, 6.8 us)
Sparse Core Ops, SparseCore 0:
  14.1 117.6 all-gather.17
Sparse Core Ops, SparseCore 1:
  217.0 14.7 all-gather.19
  270.9 101.2 all-gather.11
  374.4 49.0 all-gather.13
  439.9 98.7 reduce-scatter.1
  540.9 86.9 all-gather.15
where the time goes:
time: 695 us; the launch traced here: 685 us
  waiting for transfers between devices  338 us (49%)
  local copies, waits for them, and re-layouts  89.8 us (13%)
  blocking collectives  83.5 us (12%)
  starting transfers between devices  64.7 us (9%)
  matrix products  60.3 us (9%)
  other arithmetic  30.7 us (4%)
  between operations  17.7 us (3%)
    reduce_scatter x1, waiting for transfers between devices, on_device(): lax.psum_scatter(expert_slice(pooled, weight_in, weight_out).astype(jnp.b...  86.9 us
    all_gather x1, waiting for transfers between devices, on_device(): lax.all_gather(arrived, 'dp', axis=0, tiled=True).reshape(-1, width)  85.6 us
    all_gather x3, waiting for transfers between devices, entering(): lax.all_gather(part.astype(kind), axis)  76.3 us
    unnamed x2, blocking collectives  68.5 us
    all_to_all x1, starting transfers between devices, on_device(): lax.all_to_all(send_buffer.reshape(experts_total, capacity, width), SEQ,...  55.8 us
    all_to_all x1, waiting for transfers between devices, on_device(): lax.all_to_all(send_buffer.reshape(experts_total, capacity, width), SEQ,...  48.7 us
    all_gather x1, waiting for transfers between devices, prefix(): lax.all_gather(a.astype(kind), axis)  40.3 us
    dot_general x1, matrix products, expert_slice(): lax.dot_general(row_block, weight_in, (((1,), (1,)), ((), ())), preferred...  19.4 us
  transfers between devices with their start and end apart: 8, of which 5 were waited for; matrix products, arithmetic and copies ran while one was open for 18% of the time, Pallas kernels for 0%

commit v1 on v0

v1 whole, which is shorter than its diff:
```python
import functools
import jax
import jax.numpy as jnp
from jax import lax
from jax.experimental import pallas as pl
from jax.experimental.pallas import tpu as pltpu
from jax.sharding import PartitionSpec as P

MESH = pl.DeviceIdType.MESH
BF = jnp.bfloat16
F32 = jnp.float32
HOP = 13


def greet(ndp, nseq, dp, me):
    barrier = pltpu.get_barrier_semaphore()

    def plane(d, carry):
        pl.semaphore_signal(
            barrier, inc=1, device_id=(dp, lax.rem(me + HOP * d, nseq)), device_id_type=MESH
        )
        return carry

    for j in range(1, ndp):
        pl.semaphore_signal(
            barrier, inc=1, device_id=(lax.rem(dp + j, ndp), me), device_id_type=MESH
        )
    lax.fori_loop(1, nseq, plane, 0)
    pl.semaphore_wait(barrier, nseq - 1 + ndp - 1)


def push(src, dst, send, recv, z, e):
    pltpu.make_async_remote_copy(
        src_ref=src, dst_ref=dst, send_sem=send, recv_sem=recv, device_id=(z, e), device_id_type=MESH
    ).start()


def landed(ref, sem):
    pltpu.make_async_copy(ref, ref, sem).wait()


def interleave(n_first, n_second, first, second):
    both = min(n_first, n_second)

    def pair(i, carry):
        first(i)
        second(i)
        return carry

    def rest(i, carry):
        (first if n_first > n_second else second)(i)
        return carry

    lax.fori_loop(0, both, pair, 0)
    lax.fori_loop(both, max(n_first, n_second), rest, 0)


def each(n, body):
    def step(i, carry):
        body(i)
        return carry

    lax.fori_loop(0, n, step, 0)


def vmem(*shape, kind=BF):
    return pltpu.VMEM(shape, kind)


HEADS_AT_ONCE = 4


def ramp(run, h):
    size = run.shape[1]
    across = jnp.broadcast_to(run[pl.ds(h, 1), :], (size, size))
    down = jnp.transpose(across)
    return across, down


def lower(size):
    return lax.broadcasted_iota(jnp.int32, (size, size), 0) >= lax.broadcasted_iota(
        jnp.int32, (size, size), 1
    )


def head_span(h, head):
    return pl.ds(pl.multiple_of(h * head, head), head)


def outer(a, b):
    return lax.dot_general(a, b, (((0,), (0,)), ((), ())), preferred_element_type=F32)


def inner(a, b):
    return lax.dot_general(a, b, (((1,), (1,)), ((), ())), preferred_element_type=F32)


def attention_kernel(
    cfg, q, k, v, g, run, gain, attn_out, normed, back, core, fsend, frecv, fout, fin, bsend, brecv,
    fs, fr, gs, gr, bs, br,
):
    ndp, nseq, head = cfg
    tokens = q.shape[0]
    scale = 1.0 / head
    dp = lax.axis_index("dp")
    me = lax.axis_index("seq")
    greet(1, nseq, dp, me)

    def heads(body):
        def group(i, carry):
            for u in range(HEADS_AT_ONCE):
                body(lax.rem(me + HOP * (i * HEADS_AT_ONCE + u), nseq))
            return carry

        lax.fori_loop(0, nseq // HEADS_AT_ONCE, group, 0)

    def forward_local(h):
        cols = head_span(h, head)
        across, down = ramp(run, h)
        total = across[0:1, tokens - 1 : tokens]
        tail = jnp.exp(total - down)
        lifted = (k[:, cols].astype(F32) * tail).astype(BF)
        fsend[h, pl.ds(0, head)] = outer(lifted, v[:, cols]).astype(BF)
        decay = jnp.broadcast_to(jnp.exp(total), (8, head))
        high = decay.astype(BF)
        fsend[h, pl.ds(head, 8)] = high
        fsend[h, pl.ds(head + 8, 8)] = (decay - high.astype(F32)).astype(BF)

        @pl.when(h != me)
        def _():
            push(fsend.at[h], frecv.at[me], fs, fr, dp, h)

    heads(forward_local)
    frecv[me] = fsend[me]
    mask = lower(tokens)

    def inside(h):
        cols = head_span(h, head)
        across, down = ramp(run, h)
        weight = jnp.where(mask, jnp.exp(jnp.where(mask, down - across, 0.0)), 0.0)
        probs = (inner(q[:, cols], k[:, cols]) * weight * scale).astype(BF)
        core[:, cols] = jnp.dot(probs, v[:, cols], preferred_element_type=F32)

    heads(inside)

    def backward_local(h):
        cols = head_span(h, head)
        across, down = ramp(run, h)
        lifted = (q[:, cols].astype(F32) * jnp.exp(down)).astype(BF)
        bsend[h] = outer(lifted, g[:, cols]).astype(BF)

    heads(backward_local)
    landed(frecv.at[pl.ds(0, nseq - 1)], fr)

    def decay_of(i):
        pair = frecv[i, pl.ds(head, 16)].astype(F32)
        return pair[0:1] + pair[8:9]

    def forward_scan(i, state):
        fout[i] = state.astype(BF)

        @pl.when(i != me)
        def _():
            push(fout.at[i], fin.at[me], gs, gr, dp, i)

        return decay_of(i) * state + frecv[i, pl.ds(0, head)].astype(F32)

    lax.fori_loop(0, nseq, forward_scan, jnp.zeros((head, head), F32))
    fin[me] = fout[me]

    def backward_push(d, carry):
        h = lax.rem(me + HOP * d, nseq)
        push(bsend.at[h], brecv.at[me], bs, br, dp, h)
        return carry

    lax.fori_loop(1, nseq, backward_push, 0)
    brecv[me] = bsend[me]
    landed(fin.at[pl.ds(0, nseq - 1)], gr)

    def join(i, square):
        for u in range(HEADS_AT_ONCE):
            h = i * HEADS_AT_ONCE + u
            cols = head_span(h, head)
            across, down = ramp(run, h)
            far = jnp.dot(q[:, cols], fin[h], preferred_element_type=F32)
            total = (core[:, cols] + scale * jnp.exp(down) * far).astype(BF)
            attn_out[:, cols] = total
            wide = total.astype(F32)
            square = square + wide * wide
        return square

    square = lax.fori_loop(0, nseq // HEADS_AT_ONCE, join, jnp.zeros((tokens, head), F32))
    mean = jnp.sum(square, axis=1, keepdims=True) * (1.0 / q.shape[1])
    factor = lax.rsqrt(mean + norm_eps)

    def norm(h):
        cols = head_span(h, head)
        normed[:, cols] = (attn_out[:, cols].astype(F32) * factor * gain[:, cols]).astype(BF)

    each(nseq, norm)
    landed(brecv.at[pl.ds(0, nseq - 1)], br)

    def backward_scan(j, state):
        i = nseq - 1 - j
        back[i] = state.astype(BF)
        return decay_of(i) * state + brecv[i].astype(F32)

    lax.fori_loop(0, nseq, backward_scan, jnp.zeros((head, head), F32))
    landed(fsend.at[pl.ds(0, nseq - 1)], fs)
    landed(fout.at[pl.ds(0, nseq - 1)], gs)
    landed(bsend.at[pl.ds(0, nseq - 1)], bs)


def gradients(head, q, k, v, g, run, factor, back_in, key_out, value_out, count):
    tokens = q.shape[0]
    scale = 1.0 / head
    mask = lower(tokens)

    def group(i, carry):
        for u in range(HEADS_AT_ONCE):
            h = i * HEADS_AT_ONCE + u
            cols = head_span(h, head)
            across, down = ramp(run, h)
            tail = jnp.exp(across[0:1, tokens - 1 : tokens] - down) * scale
            weight = jnp.where(mask, jnp.exp(jnp.where(mask, down - across, 0.0)), 0.0)
            qh, kh, vh, gh = q[:, cols], k[:, cols], v[:, cols], g[:, cols]
            state = back_in[h]
            power = factor[pl.ds(h, 1), :]
            probs = (inner(qh, kh) * weight * scale).astype(BF)
            pulled = (inner(gh, vh) * weight * scale).astype(BF)
            key_grad = outer(pulled, qh) + tail * inner(vh, state)
            value_grad = outer(probs, gh) + tail * jnp.dot(kh, state, preferred_element_type=F32)
            key_out[:, cols] = (key_grad * power).astype(BF)
            value_out[:, cols] = (value_grad * power).astype(BF)
        return carry

    lax.fori_loop(0, count // HEADS_AT_ONCE, group, 0)


def attention(q, k, v, g, run, gain, ndp, nseq, head):
    tokens, model = q.shape
    dma = pltpu.SemaphoreType.DMA
    whole = pl.BlockSpec(memory_space=pltpu.VMEM)
    return pl.pallas_call(
        functools.partial(attention_kernel, (ndp, nseq, head)),
        out_shape=(
            jax.ShapeDtypeStruct((tokens, model), BF),
            jax.ShapeDtypeStruct((tokens, model), BF),
            jax.ShapeDtypeStruct((nseq, head, head), BF),
        ),
        in_specs=[whole] * 6,
        out_specs=(whole,) * 3,
        scratch_shapes=[
            vmem(tokens, model, kind=F32),
            vmem(nseq, head + 16, head),
            vmem(nseq, head + 16, head),
            vmem(nseq, head, head),
            vmem(nseq, head, head),
            vmem(nseq, head, head),
            vmem(nseq, head, head),
            dma, dma, dma, dma, dma, dma,
        ],
        compiler_params=pltpu.CompilerParams(
            collective_id=0, has_side_effects=True, vmem_limit_bytes=40 << 20
        ),
        name="attention",
    )(q, k, v, g, run, gain)


def dispatch_kernel(
    cfg, normed, meta, w_in, q, k, v, g, run, factor, back, hid, meta_all, key_out, value_out,
    x, send_a, send_b, tok, mets, onehot, wv, acc, back_in,
    wsem, ms, mr, ts, tr, as_, ar, bs, br, fs, fr, gs, gr,
):
    ndp, nseq, cap, width, n_a, n_b = cfg
    head = back.shape[1]
    ca = n_a * width
    rows = nseq * cap
    dp = lax.axis_index("dp")
    me = lax.axis_index("seq")
    near = (1, ndp - 1) + tuple(range(2, ndp - 1))

    def span(i, start=0):
        return pl.ds(pl.multiple_of(start + i * width, width), width)

    load_w = pltpu.make_async_copy(w_in.at[0], wv, wsem)
    load_w.start()
    greet(ndp, nseq, dp, me)
    for j in range(1, ndp):
        push(meta, mets.at[dp], ms, mr, lax.rem(dp + j, ndp), me)

    def give(c):
        for j in near:
            z = lax.rem(dp + j, ndp)
            push(normed.at[:, span(c, ca)], tok.at[dp, :, span(c)], ts, tr.at[c], z, me)

    each(n_b, give)

    def spread(d, carry):
        i = lax.rem(me + HOP * d, nseq)
        push(back.at[i], back_in.at[me], gs, gr, dp, i)
        return carry

    lax.fori_loop(1, nseq, spread, 0)
    back_in[me] = back[me]
    mets[dp] = meta[...]

    def select(z):
        slots = lax.broadcasted_iota(jnp.int32, (rows, meta.shape[1]), 0).astype(F32)
        m = mets[z]
        hit = (slots == m[0:1]) | (slots == m[1:2])
        onehot[z] = jnp.where(hit, 1.0, 0.0).astype(BF)

    select(dp)

    def plane_a(a):
        cols = span(a)
        part = jnp.dot(onehot[dp], normed[:, cols], preferred_element_type=F32).astype(BF)
        send_a[:, :, :, cols] = part.reshape(nseq, cap // 2, 2, width)
        x[dp, me, :, :, cols] = send_a[me, :, :, cols]

        def go(d, carry):
            e = lax.rem(me + HOP * d, nseq)
            push(send_a.at[e, :, :, cols], x.at[dp, me, :, :, cols], as_, ar.at[a], dp, e)
            return carry

        lax.fori_loop(1, nseq, go, 0)

    each(n_a, plane_a)

    def own(c):
        tok[dp, :, span(c)] = normed[:, span(c, ca)]

    each(n_b, own)
    landed(mets.at[pl.ds(0, ndp - 1)], mr)
    for j in range(1, ndp):
        select(lax.rem(dp + j, ndp))

    def plane_b(i):
        cols, there = span(i), span(i, ca)
        landed(tok.at[pl.ds(0, ndp - 1), :, cols], tr.at[i])

        def build(z):
            part = jnp.dot(onehot[z], tok[z, :, cols], preferred_element_type=F32).astype(BF)
            send_b[z, :, :, :, cols] = part.reshape(nseq, cap // 2, 2, width)
            x[z, me, :, :, there] = send_b[z, me, :, :, cols]

        each(ndp, build)

        def go(d, carry):
            e = lax.rem(me + HOP * d, nseq)
            push(send_b.at[:, e, :, :, cols], x.at[:, me, :, :, there], bs, br.at[i], dp, e)
            return carry

        lax.fori_loop(1, nseq, go, 0)

    def onward_a(i):
        cols = span(i)
        landed(x.at[dp, pl.ds(0, nseq - 1), :, :, cols], ar.at[i])
        for j in near:
            z = lax.rem(dp + j, ndp)
            push(x.at[dp, :, :, :, cols], x.at[dp, :, :, :, cols], fs, fr.at[i], z, me)

    interleave(n_b, n_a, plane_b, onward_a)

    landed(back_in.at[pl.ds(0, nseq - 1)], gr)
    gradients(head, q, k, v, g, run, factor, back_in, key_out, value_out, nseq)

    def clear(z):
        here = pl.ds(pl.multiple_of(z * rows, rows), rows)
        acc[here] = jnp.zeros((rows, acc.shape[1]), F32)

    each(ndp, clear)
    load_w.wait()

    def absorb(cols):
        def part(z):
            block = x[z, :, :, :, cols].reshape(rows, width)
            here = pl.ds(pl.multiple_of(z * rows, rows), rows)
            acc[here] += lax.dot_general(
                block, wv[:, cols], (((1,), (1,)), ((), ())), preferred_element_type=F32
            )

        each(ndp, part)

    def absorb_b(i):
        cols = span(i, ca)
        landed(x.at[:, pl.ds(0, nseq - 1), :, :, cols], br.at[i])
        absorb(cols)

    def absorb_a(i):
        cols = span(i)
        landed(x.at[pl.ds(0, ndp - 1), :, :, :, cols], fr.at[i])
        absorb(cols)

    interleave(n_b, n_a, absorb_b, absorb_a)

    def finish(z):
        here = pl.ds(pl.multiple_of(z * rows, rows), rows)
        hid[here] = jax.nn.silu(acc[here]).astype(BF)

    each(ndp, finish)
    meta_all[...] = mets[...]
    landed(back.at[pl.ds(0, nseq - 1)], gs)
    landed(mets.at[pl.ds(0, ndp - 1)], ms)
    if n_b:
        landed(tok.at[pl.ds(0, ndp - 1)], ts)
        landed(send_b.at[:, pl.ds(0, nseq - 1)], bs)
    if n_a:
        landed(send_a.at[pl.ds(0, nseq - 1)], as_)
        landed(x.at[pl.ds(0, ndp - 1), :, :, :, pl.ds(0, ca)], fs)


def combine_kernel(
    cfg, hid, meta_all, w_out, base, out, own_a, part_b, from_z, send_a, ret_a, ret_b, sums, got, mix, wv,
    wsem, zs, zr, bs, br, as_, ar, ss, sr,
):
    ndp, nseq, cap, width, n_a, n_b = cfg
    ca = n_a * width
    rows = nseq * cap
    tokens = base.shape[0]
    dp = lax.axis_index("dp")
    me = lax.axis_index("seq")
    near = (1, ndp - 1) + tuple(range(2, ndp - 1))

    def span(i, start=0):
        return pl.ds(pl.multiple_of(start + i * width, width), width)

    def fetch(cols, c):
        return pltpu.make_async_copy(w_out.at[0, :, cols], wv.at[:, cols], wsem.at[c])

    interleave(
        n_b, n_a,
        lambda i: fetch(span(i, ca), n_a + i).start(),
        lambda i: fetch(span(i), i).start(),
    )
    greet(ndp, nseq, dp, me)

    def second(z, cols):
        here = pl.ds(pl.multiple_of(z * rows, rows), rows)
        y = jnp.dot(hid[here], wv[:, cols], preferred_element_type=F32)
        return y.astype(BF).reshape(nseq, cap // 2, 2, width)

    def make_b(i):
        cols, there = span(i), span(i, ca)
        fetch(there, n_a + i).wait()

        def part(z):
            part_b[z, :, :, :, cols] = second(z, there)
            ret_b[z, me, :, :, cols] = part_b[z, me, :, :, cols]

        each(ndp, part)

        def go(d, carry):
            e = lax.rem(me + HOP * d, nseq)
            push(part_b.at[:, e, :, :, cols], ret_b.at[:, me, :, :, cols], bs, br.at[i], dp, e)
            return carry

        lax.fori_loop(1, nseq, go, 0)

    def make_a(i):
        cols = span(i)
        fetch(cols, i).wait()

        def part(z):
            own_a[z, :, :, :, cols] = second(z, cols)

        each(ndp, part)
        for j in near:
            z = lax.rem(dp + j, ndp)
            push(own_a.at[z, :, :, :, cols], from_z.at[dp, :, :, :, cols], zs, zr.at[i], z, me)

    interleave(n_b, n_a, make_b, make_a)

    eye = jnp.where(
        lax.broadcasted_iota(jnp.int32, (tokens, tokens), 0)
        == lax.broadcasted_iota(jnp.int32, (tokens, tokens), 1), 1.0, 0.0,
    ).astype(BF)

    def weigh(z):
        slots = lax.broadcasted_iota(jnp.int32, (rows, tokens), 0).astype(F32)
        m = meta_all[z]
        pick = jnp.where(slots == m[0:1], m[2:3], 0.0) + jnp.where(slots == m[1:2], m[3:4], 0.0)
        mix[z] = lax.dot_general(
            eye, pick.astype(BF), (((1,), (1,)), ((), ())), preferred_element_type=F32
        ).astype(BF)

    each(ndp, weigh)

    def back_a(i):
        cols = span(i)
        landed(from_z.at[pl.ds(0, ndp - 1), :, :, :, cols], zr.at[i])

        def add(e, carry):
            some = pl.ds(e * 4, 4)
            flat = (4 * cap, width)
            total = own_a[dp, some, :, :, cols].reshape(flat).astype(F32)
            for j in range(1, ndp):
                z = lax.rem(dp + j, ndp)
                total = total + from_z[z, some, :, :, cols].reshape(flat).astype(F32)
            send_a[some, :, :, cols] = total.astype(BF).reshape(4, cap // 2, 2, width)
            return carry

        lax.fori_loop(0, nseq // 4, add, 0)
        ret_a[me, :, :, cols] = send_a[me, :, :, cols]

        def go(d, carry):
            e = lax.rem(me + HOP * d, nseq)
            push(send_a.at[e, :, :, cols], ret_a.at[me, :, :, cols], as_, ar.at[i], dp, e)
            return carry

        lax.fori_loop(1, nseq, go, 0)

    def mix_b(i):
        cols = span(i)
        landed(ret_b.at[:, pl.ds(0, nseq - 1), :, :, cols], br.at[i])

        def part(z):
            block = ret_b[z, :, :, :, cols].reshape(rows, width)
            sums[z, :, cols] = jnp.dot(mix[z], block, preferred_element_type=F32).astype(BF)

        each(ndp, part)
        for j in near:
            z = lax.rem(dp + j, ndp)
            push(sums.at[z, :, cols], got.at[dp, :, cols], ss, sr.at[i], z, me)

    interleave(n_b, n_a, mix_b, back_a)

    def end_a(i):
        cols = span(i)
        landed(ret_a.at[pl.ds(0, nseq - 1), :, :, cols], ar.at[i])
        block = ret_a[:, :, :, cols].reshape(rows, width)
        mixed = jnp.dot(mix[dp], block, preferred_element_type=F32)
        out[:, cols] = (base[:, cols].astype(F32) + mixed).astype(BF)

    def end_b(i):
        cols, there = span(i), span(i, ca)
        landed(got.at[pl.ds(0, ndp - 1), :, cols], sr.at[i])
        total = sums[dp, :, cols].astype(F32)
        for j in range(1, ndp):
            total = total + got[lax.rem(dp + j, ndp), :, cols].astype(F32)
        out[:, there] = (base[:, there].astype(F32) + total).astype(BF)

    interleave(n_b, n_a, end_b, end_a)
    if n_a:
        landed(own_a.at[pl.ds(0, ndp - 1)], zs)
        landed(send_a.at[pl.ds(0, nseq - 1)], as_)
    if n_b:
        landed(part_b.at[:, pl.ds(0, nseq - 1)], bs)
        landed(sums.at[pl.ds(0, ndp - 1)], ss)


def experts(
    normed, base, q, k, v, g, run, factor, back, choice, slot, weights, w_in, w_out, ndp, nseq, cap, split
):
    tokens, model = normed.shape
    hidden = w_in.shape[1]
    n_a, n_b, width = split
    rows = nseq * cap
    ca, cb = n_a * width, n_b * width
    cfg = (ndp, nseq, cap, width, n_a, n_b)
    target = (choice * cap + slot).astype(F32).T
    meta = jnp.concatenate([target, weights.T, jnp.zeros((4, tokens), F32)], axis=0)
    dma = pltpu.SemaphoreType.DMA
    whole = pl.BlockSpec(memory_space=pltpu.VMEM)
    away = pl.BlockSpec(memory_space=pl.ANY)
    hid, meta_all, key_out, value_out = pl.pallas_call(
        functools.partial(dispatch_kernel, cfg),
        out_shape=(
            jax.ShapeDtypeStruct((ndp * rows, hidden), BF),
            jax.ShapeDtypeStruct((ndp, 8, tokens), F32),
            jax.ShapeDtypeStruct((tokens, model), BF),
            jax.ShapeDtypeStruct((tokens, model), BF),
        ),
        in_specs=[whole, whole, away] + [whole] * 7,
        out_specs=(whole,) * 4,
        scratch_shapes=[
            vmem(ndp, nseq, cap // 2, 2, model),
            vmem(nseq, cap // 2, 2, max(ca, 128)),
            vmem(ndp, nseq, cap // 2, 2, max(cb, 128)),
            vmem(ndp, tokens, max(cb, 128)),
            vmem(ndp, 8, tokens, kind=F32),
            vmem(ndp, rows, tokens),
            vmem(hidden, model),
            vmem(ndp * rows, hidden, kind=F32),
            vmem(*back.shape),
            dma, dma, dma, dma, dma((max(n_b, 1),)), dma, dma((max(n_a, 1),)),
            dma, dma((max(n_b, 1),)), dma, dma((max(n_a, 1),)), dma, dma,
        ],
        compiler_params=pltpu.CompilerParams(
            collective_id=1, has_side_effects=True, vmem_limit_bytes=62 << 20
        ),
        name="dispatch",
    )(normed, meta, w_in, q, k, v, g, run, factor, back)
    layer_out = pl.pallas_call(
        functools.partial(combine_kernel, cfg),
        out_shape=jax.ShapeDtypeStruct((tokens, model), BF),
        in_specs=[whole, whole, away, whole],
        out_specs=whole,
        scratch_shapes=[
            vmem(ndp, nseq, cap // 2, 2, max(ca, 128)),
            vmem(ndp, nseq, cap // 2, 2, max(cb, 128)),
            vmem(ndp, nseq, cap // 2, 2, max(ca, 128)),
            vmem(nseq, cap // 2, 2, max(ca, 128)),
            vmem(nseq, cap // 2, 2, max(ca, 128)),
            vmem(ndp, nseq, cap // 2, 2, max(cb, 128)),
            vmem(ndp, tokens, max(cb, 128)),
            vmem(ndp, tokens, max(cb, 128)),
            vmem(ndp, tokens, rows),
            vmem(hidden, model),
            dma((n_a + n_b,)), dma, dma((max(n_a, 1),)), dma, dma((max(n_b, 1),)),
            dma, dma((max(n_a, 1),)), dma, dma((max(n_b, 1),)),
        ],
        compiler_params=pltpu.CompilerParams(
            collective_id=2, has_side_effects=True, vmem_limit_bytes=62 << 20
        ),
        name="combine",
    )(hid, meta_all, w_out, base)
    return layer_out, key_out, value_out


norm_eps = 1e-06
TOP = 2
SPLIT = (4, 4, 512)


def on_device(
    queries, keys, values, log_decay, attn_grad, norm_gain, route_ids, route_weights, grad_exponent,
    w_in, w_out,
):
    length, width = queries.shape[1:]
    ndp, nseq = lax.axis_size("dp"), lax.axis_size("seq")
    heads = log_decay.shape[1]
    head = width // heads
    cap = max(2, TOP * length * 5 // (4 * nseq))
    run = jnp.cumsum(log_decay[0], axis=1)
    factor = jnp.broadcast_to(jnp.exp2(grad_exponent.astype(F32))[:, None], (heads, head))
    choice = route_ids[0]
    flat = choice.reshape(length * TOP)
    onehot = (flat[:, None] == jnp.arange(nseq, dtype=jnp.int32)[None, :]).astype(jnp.int32)
    slot = jnp.sum((jnp.cumsum(onehot, axis=0) - 1) * onehot, axis=-1).reshape(length, TOP)
    q, k, v, g = queries[0], keys[0], values[0], attn_grad[0]
    attn_out, normed, back = attention(q, k, v, g, run, norm_gain[None], ndp, nseq, head)
    layer_out, key_out, value_out = experts(
        normed, attn_out, q, k, v, g, run, factor, back, choice, slot, route_weights[0], w_in, w_out,
        ndp, nseq, cap, SPLIT,
    )
    return (layer_out[None], key_out[None], value_out[None])


def solution(mesh):
    rows = P("dp", "seq", None)
    placed = (
        rows, rows, rows, P("dp", None, "seq"), rows, P(), rows, rows, P(),
        P("seq", "dp", None), P("seq", "dp", None),
    )
    return jax.shard_map(
        on_device, mesh=mesh, in_specs=placed, out_specs=(rows, rows, rows), check_vma=False
    )
```

time: 695 us -> 274 us (0.39); the launches traced: 685 us -> 273 us
  waiting for transfers between devices: 338 us -> 0 us
  Pallas kernels: 0 us -> 252 us
  blocking collectives: 83.5 us -> 0 us
  local copies, waits for them, and re-layouts: 89.8 us -> 16.3 us
  starting transfers between devices: 64.7 us -> 0 us
  matrix products: 60.3 us -> 0 us
  other arithmetic: 30.7 us -> 4.44 us
  between operations: 17.7 us -> 0.71 us
    pallas_call x0 -> x3, Pallas kernels: none -> 252 us  [the longest x1 103 us: experts(): pl.pallas_call(functools.partial(dispatch_kernel, cfg), out_shape=(jax.Sh...]
    all_gather x5 -> x0, waiting for transfers between devices: 202 us -> none  [the longest x1 85.6 us: on_device(): lax.all_gather(arrived, 'dp', axis=0, tiled=True).reshape(-1, width)]
    reduce_scatter x1 -> x0, waiting for transfers between devices: 86.9 us -> none  [on_device(): lax.psum_scatter(expert_slice(pooled, weight_in, weight_out).astype(jnp.b...]
    unnamed x2 -> x0, blocking collectives: 68.5 us -> none
    all_to_all x2 -> x0, starting transfers between devices: 64 us -> none  [the longest x1 55.8 us: on_device(): lax.all_to_all(send_buffer.reshape(experts_total, capacity, width), SEQ,...]
    dot_general x11 -> x0, matrix products: 60.3 us -> none  [the longest x1 19.4 us: expert_slice(): lax.dot_general(row_block, weight_in, (((1,), (1,)), ((), ())), preferred...]
    all_to_all x2 -> x0, waiting for transfers between devices: 48.7 us -> none  [the longest x1 48.7 us: on_device(): lax.all_to_all(send_buffer.reshape(experts_total, capacity, width), SEQ,...]
    reshape x5 -> x2, local copies, waits for them, and re-layouts: 31.6 us -> 0.2 us  [on_device(): jnp.sum((jnp.cumsum(onehot, axis=0) - 1) * onehot, axis=-1)]
  transfers between devices with their start and end apart: 8 -> 0, of which waited for: 5 -> 0; matrix products, arithmetic and copies ran while one was open for 18% -> 0% of each run, Pallas kernels for 0% -> 0%
where the time goes in v1:
time: 274 us; the launch traced here: 273 us
  Pallas kernels  252 us (92%)
  local copies, waits for them, and re-layouts  16.3 us (6%)
  other arithmetic  4.44 us (2%)
    pallas_call x1, Pallas kernels, experts(): pl.pallas_call(functools.partial(dispatch_kernel, cfg), out_shape=(jax.Sh...  103 us
    pallas_call x1, Pallas kernels, experts(): pl.pallas_call(functools.partial(combine_kernel, cfg), out_shape=jax.Shap...  96.2 us
    pallas_call x1, Pallas kernels, attention(): pl.pallas_call(functools.partial(attention_kernel, (ndp, nseq, head)), ou...  53.1 us
    unnamed x24, local copies, waits for them, and re-layouts  14.9 us

profile of v1, /device:TPU:1, one launch (start us, length us, event | category | flops | bytes accessed | tf_op | source)
XLA Modules:
  0.0 273.4 jit_solution(868800196868709063)
XLA Ops:
  0.6 0.7 multiply_exponential_fusion
  1.4 0.7 broadcast_in_dim.24.factor
  2.0 1.0 reduce_window_sum.24.run
  3.0 0.8 copy.14
  4.0 0.1 eq.25
  4.1 0.6 reduce-window.6
  4.7 0.2 slice_reduce_fusion
  5.1 0.1 reshape.32
  5.3 0.7 fusion.4
  6.0 1.3 maximum_maximum_fusion.meta
  7.3 1.2 copy-done
  8.5 1.2 copy-done.1
  9.8 1.2 copy-done.2
  11.0 1.2 copy-done.3
  12.2 0.7 copy-done.8
  12.9 53.1 %attention.1 = (bf16[128,4096]{1,0:T(8,128)(2,1)S(1)}, bf16[128,4096]{1,0:T(8,128)(2,1)S(1)}, bf16[32,128,128]{2,1,0:T(8,128)(2,1)S(1)}) custom-call(bf16[128,4096]{1,0:T(8,128)(2,1)S(1)} %bitcast.36, bf16[128,4096]{1,0:T(8,128)(2,1)S(1)} %bitcast.38, bf16[128,4096]{1,0:T(8,128)(2,1)S(1)} %bitcast.40, bf16[128,4096]{1,0:T(8,128)(2,1)S(1)} %bitcast.42, ...), custom_call_target="tpu_custom_call" | custom-call | tf_op jit(solution)/shard_map/attention/pallas_call | solution.py:244
  66.1 1.0 copy-done.4
  67.0 1.0 copy-done.5
  68.0 1.0 copy-done.6
  69.0 102.6 %dispatch.1 = (bf16[1280,1152]{1,0:T(8,128)(2,1)}, f32[4,8,128]{2,1,0:T(8,128)}, bf16[128,4096]{1,0:T(8,128)(2,1)}, bf16[128,4096]{1,0:T(8,128)(2,1)}) custom-call(bf16[128,4096]{1,0:T(8,128)(2,1)} %copy-done.4, f32[8,128]{1,0:T(8,128)} %maximum_maximum_fusion.meta, bf16[1,1152,4096]{2,1,0:T(8,128)(2,1)} %w_in.1, bf16[128,4096]{1,0:T(8,128)(2,1)} %bitcast.35, ...), custom_call_target="tpu_custom_call" | custom-call | tf_op jit(solution)/shard_map/dispatch/pallas_call | solution.py:567
  171.6 96.2 %combine.1 = bf16[128,4096]{1,0:T(8,128)(2,1)} custom-call(bf16[1280,1152]{1,0:T(8,128)(2,1)} %get-tuple-element.12.hid, f32[4,8,128]{2,1,0:T(8,128)} %get-tuple-element.13.meta_all, bf16[1,1152,4096]{2,1,0:T(8,128)(2,1)} %w_out.1, bf16[128,4096]{1,0:T(8,128)(2,1)} %copy-done.6), custom_call_target="tpu_custom_call" | custom-call | tf_op jit(solution)/shard_map/combine/pallas_call | solution.py:595
  267.8 2.3 copy.23
  270.1 2.3 copy.24
  272.4 1.0 copy.25
  (20 shorter events, 0.4 us)
Async XLA Ops:
  3.0 65.9 %copy-start.7 = (f32[32,128]{1,0:T(8,128)}, f32[32,128]{1,0:T(8,128)S(1)}, u32[]{:S(2)}) copy-start(f32[32,128]{1,0:T(8,128)S(1)} %reduce_window_sum.24.run) | copy-start | bytes 49156
  7.3 1.2 copy-start
  8.5 1.2 copy-start.1
  9.8 1.2 copy-start.2
  11.0 1.2 copy-start.3
  12.2 0.7 copy-start.8
  66.1 1.0 copy-start.4
  67.0 1.0 copy-start.5
  68.0 1.0 copy-start.6
  171.6 100.8 %copy-start.9 = (bf16[128,4096]{1,0:T(8,128)(2,1)S(1)}, bf16[128,4096]{1,0:T(8,128)(2,1)}, u32[]{:S(2)}) copy-start(bf16[128,4096]{1,0:T(8,128)(2,1)} %get-tuple-element.16) | copy-start | bytes 3145732

commit v2 on v1

--- a/solution.py
+++ b/solution.py
@@ -96,15 +96,30 @@
 
 
 def attention_kernel(
-    cfg, q, k, v, g, run, gain, attn_out, normed, back, core, fsend, frecv, fout, fin, bsend, brecv,
-    fs, fr, gs, gr, bs, br,
+    cfg, q_far, k_far, v_far, g_far, decay, gain, ids, weights, attn_out, normed, back, run, meta,
+    q, k, v, g, core, fsend, frecv, fout, fin, bsend, brecv, ls, fs, fr, gs, gr, bs, br,
 ):
-    ndp, nseq, head = cfg
+    ndp, nseq, head, cap = cfg
     tokens = q.shape[0]
     scale = 1.0 / head
     dp = lax.axis_index("dp")
     me = lax.axis_index("seq")
+    loads = [
+        pltpu.make_async_copy(far.at[0], near, ls.at[n])
+        for n, (far, near) in enumerate(((k_far, k), (v_far, v), (q_far, q), (g_far, g)))
+    ]
+    for load in loads:
+        load.start()
+    sums = decay[0]
+    lane = lax.broadcasted_iota(jnp.int32, sums.shape, 1)
+    step = 1
+    while step < tokens:
+        sums = sums + jnp.where(lane >= step, pltpu.roll(sums, step, 1), 0.0)
+        step *= 2
+    run[...] = sums
     greet(1, nseq, dp, me)
+    loads[0].wait()
+    loads[1].wait()
 
     def heads(body):
         def group(i, carry):
@@ -133,6 +148,17 @@
     heads(forward_local)
     frecv[me] = fsend[me]
     mask = lower(tokens)
+    first, second = ids[0, 0:1], ids[0, 1:2]
+    owner = lax.broadcasted_iota(jnp.int32, (nseq, tokens), 0)
+    named = ((owner == first) | (owner == second)).astype(F32).astype(BF)
+    before = jnp.where(mask, 0.0, 1.0).astype(BF)
+    slots = jnp.dot(named, before, preferred_element_type=F32) + (owner * cap).astype(F32)
+    for row, choice in enumerate((first, second)):
+        meta[row : row + 1] = jnp.sum(jnp.where(owner == choice, slots, 0.0), axis=0, keepdims=True)
+    meta[2:4] = weights[0]
+    meta[4:8] = jnp.zeros((4, tokens), F32)
+    loads[2].wait()
+    loads[3].wait()
 
     def inside(h):
         cols = head_span(h, head)
@@ -237,20 +263,27 @@
     lax.fori_loop(0, count // HEADS_AT_ONCE, group, 0)
 
 
-def attention(q, k, v, g, run, gain, ndp, nseq, head):
-    tokens, model = q.shape
+def attention(q, k, v, g, decay, gain, ids, weights, ndp, nseq, head, cap):
+    tokens, model = q.shape[1:]
     dma = pltpu.SemaphoreType.DMA
     whole = pl.BlockSpec(memory_space=pltpu.VMEM)
+    away = pl.BlockSpec(memory_space=pl.ANY)
     return pl.pallas_call(
-        functools.partial(attention_kernel, (ndp, nseq, head)),
+        functools.partial(attention_kernel, (ndp, nseq, head, cap)),
         out_shape=(
             jax.ShapeDtypeStruct((tokens, model), BF),
             jax.ShapeDtypeStruct((tokens, model), BF),
             jax.ShapeDtypeStruct((nseq, head, head), BF),
+            jax.ShapeDtypeStruct((nseq, tokens), F32),
+            jax.ShapeDtypeStruct((8, tokens), F32),
         ),
-        in_specs=[whole] * 6,
-        out_specs=(whole,) * 3,
+        in_specs=[away] * 4 + [whole] * 4,
+        out_specs=(whole,) * 5,
         scratch_shapes=[
+            vmem(tokens, model),
+            vmem(tokens, model),
+            vmem(tokens, model),
+            vmem(tokens, model),
             vmem(tokens, model, kind=F32),
             vmem(nseq, head + 16, head),
             vmem(nseq, head + 16, head),
@@ -258,19 +291,20 @@
             vmem(nseq, head, head),
             vmem(nseq, head, head),
             vmem(nseq, head, head),
-            dma, dma, dma, dma, dma, dma,
+            dma((4,)), dma, dma, dma, dma, dma, dma,
         ],
         compiler_params=pltpu.CompilerParams(
-            collective_id=0, has_side_effects=True, vmem_limit_bytes=40 << 20
+            collective_id=0, has_side_effects=True, vmem_limit_bytes=62 << 20
         ),
         name="attention",
-    )(q, k, v, g, run, gain)
+    )(q, k, v, g, decay, gain, ids, weights)
 
 
 def dispatch_kernel(
-    cfg, normed, meta, w_in, q, k, v, g, run, factor, back, hid, meta_all, key_out, value_out,
-    x, send_a, send_b, tok, mets, onehot, wv, acc, back_in,
-    wsem, ms, mr, ts, tr, as_, ar, bs, br, fs, fr, gs, gr,
+    cfg, normed, meta, w_in, q_far, k_far, v_far, g_far, run, factor, back,
+    hid, meta_all, key_out, value_out,
+    x, send_a, send_b, tok, mets, onehot, wv, acc, back_in, q, k, v, g,
+    wsem, ls, ms, mr, ts, tr, as_, ar, bs, br, fs, fl, fr, hs, hl, hr, gs, gr,
 ):
     ndp, nseq, cap, width, n_a, n_b = cfg
     head = back.shape[1]
@@ -284,7 +318,15 @@
         return pl.ds(pl.multiple_of(start + i * width, width), width)
 
     load_w = pltpu.make_async_copy(w_in.at[0], wv, wsem)
+    loads = [
+        pltpu.make_async_copy(far.at[0], close, ls.at[n])
+        for n, (far, close) in enumerate(((q_far, q), (k_far, k), (v_far, v), (g_far, g)))
+    ]
     load_w.start()
+    for load in loads:
+        load.start()
+    right, left, far_z = lax.rem(dp + 1, ndp), lax.rem(dp + 3, ndp), lax.rem(dp + 2, ndp)
+    low, high = pl.ds(0, nseq // 2), pl.ds(nseq // 2, nseq // 2)
     greet(ndp, nseq, dp, me)
     for j in range(1, ndp):
         push(meta, mets.at[dp], ms, mr, lax.rem(dp + j, ndp), me)
@@ -296,13 +338,6 @@
 
     each(n_b, give)
 
-    def spread(d, carry):
-        i = lax.rem(me + HOP * d, nseq)
-        push(back.at[i], back_in.at[me], gs, gr, dp, i)
-        return carry
-
-    lax.fori_loop(1, nseq, spread, 0)
-    back_in[me] = back[me]
     mets[dp] = meta[...]
 
     def select(z):
@@ -328,6 +363,14 @@
 
     each(n_a, plane_a)
 
+    def spread(d, carry):
+        i = lax.rem(me + HOP * d, nseq)
+        push(back.at[i], back_in.at[me], gs, gr, dp, i)
+        return carry
+
+    lax.fori_loop(1, nseq, spread, 0)
+    back_in[me] = back[me]
+
     def own(c):
         tok[dp, :, span(c)] = normed[:, span(c, ca)]
 
@@ -357,41 +400,53 @@
     def onward_a(i):
         cols = span(i)
         landed(x.at[dp, pl.ds(0, nseq - 1), :, :, cols], ar.at[i])
-        for j in near:
-            z = lax.rem(dp + j, ndp)
-            push(x.at[dp, :, :, :, cols], x.at[dp, :, :, :, cols], fs, fr.at[i], z, me)
+        push(x.at[dp, :, :, :, cols], x.at[dp, :, :, :, cols], fs, fl.at[i], right, me)
+        push(x.at[dp, :, :, :, cols], x.at[dp, :, :, :, cols], fs, fr.at[i], left, me)
 
     interleave(n_b, n_a, plane_b, onward_a)
-
-    landed(back_in.at[pl.ds(0, nseq - 1)], gr)
-    gradients(head, q, k, v, g, run, factor, back_in, key_out, value_out, nseq)
 
     def clear(z):
         here = pl.ds(pl.multiple_of(z * rows, rows), rows)
         acc[here] = jnp.zeros((rows, acc.shape[1]), F32)
 
     each(ndp, clear)
+    landed(back_in.at[pl.ds(0, nseq - 1)], gr)
+    for load in loads:
+        load.wait()
+    gradients(head, q, k, v, g, run, factor, back_in, key_out, value_out, nseq)
     load_w.wait()
 
-    def absorb(cols):
-        def part(z):
-            block = x[z, :, :, :, cols].reshape(rows, width)
-            here = pl.ds(pl.multiple_of(z * rows, rows), rows)
-            acc[here] += lax.dot_general(
-                block, wv[:, cols], (((1,), (1,)), ((), ())), preferred_element_type=F32
-            )
-
-        each(ndp, part)
+    def absorb(z, cols):
+        block = x[z, :, :, :, cols].reshape(rows, width)
+        here = pl.ds(pl.multiple_of(z * rows, rows), rows)
+        acc[here] += lax.dot_general(
+            block, wv[:, cols], (((1,), (1,)), ((), ())), preferred_element_type=F32
+        )
+
+    def relay_a(i):
+        cols = span(i)
+        landed(x.at[left, :, :, :, cols], fl.at[i])
+        push(x.at[left, low, :, :, cols], x.at[left, low, :, :, cols], hs, hl.at[i], right, me)
+        landed(x.at[right, :, :, :, cols], fr.at[i])
+        push(x.at[right, high, :, :, cols], x.at[right, high, :, :, cols], hs, hr.at[i], left, me)
+
+        def part(j):
+            absorb(lax.rem(dp + 3 + j, ndp), cols)
+
+        each(3, part)
+
+    each(n_a, relay_a)
 
     def absorb_b(i):
         cols = span(i, ca)
         landed(x.at[:, pl.ds(0, nseq - 1), :, :, cols], br.at[i])
-        absorb(cols)
+        each(ndp, lambda z: absorb(z, cols))
 
     def absorb_a(i):
         cols = span(i)
-        landed(x.at[pl.ds(0, ndp - 1), :, :, :, cols], fr.at[i])
-        absorb(cols)
+        landed(x.at[far_z, low, :, :, cols], hl.at[i])
+        landed(x.at[far_z, high, :, :, cols], hr.at[i])
+        absorb(far_z, cols)
 
     interleave(n_b, n_a, absorb_b, absorb_a)
 
@@ -408,12 +463,13 @@
         landed(send_b.at[:, pl.ds(0, nseq - 1)], bs)
     if n_a:
         landed(send_a.at[pl.ds(0, nseq - 1)], as_)
-        landed(x.at[pl.ds(0, ndp - 1), :, :, :, pl.ds(0, ca)], fs)
+        landed(x.at[pl.ds(0, 2), :, :, :, pl.ds(0, ca)], fs)
+        landed(x.at[0, :, :, :, pl.ds(0, ca)], hs)
 
 
 def combine_kernel(
-    cfg, hid, meta_all, w_out, base, out, own_a, part_b, from_z, send_a, ret_a, ret_b, sums, got, mix, wv,
-    wsem, zs, zr, bs, br, as_, ar, ss, sr,
+    cfg, hid, meta_all, w_out, base, out, own_a, part_b, half_l, half_r, from_l, from_r, send_a, ret_a, ret_b,
+    sums, got, mix, wv, wsem, zs, hl, hr, fs, fl, fr, bs, br, as_, ar, ss, sr,
 ):
     ndp, nseq, cap, width, n_a, n_b = cfg
     ca = n_a * width
@@ -430,10 +486,13 @@
         return pltpu.make_async_copy(w_out.at[0, :, cols], wv.at[:, cols], wsem.at[c])
 
     interleave(
-        n_b, n_a,
+        n_a, n_b,
+        lambda i: fetch(span(i), i).start(),
         lambda i: fetch(span(i, ca), n_a + i).start(),
-        lambda i: fetch(span(i), i).start(),
     )
+    right, left, far_z = lax.rem(dp + 1, ndp), lax.rem(dp + 3, ndp), lax.rem(dp + 2, ndp)
+    mid = nseq // 2
+    low, high = pl.ds(0, mid), pl.ds(mid, mid)
     greet(ndp, nseq, dp, me)
 
     def second(z, cols):
@@ -465,12 +524,55 @@
         def part(z):
             own_a[z, :, :, :, cols] = second(z, cols)
 
-        each(ndp, part)
-        for j in near:
-            z = lax.rem(dp + j, ndp)
-            push(own_a.at[z, :, :, :, cols], from_z.at[dp, :, :, :, cols], zs, zr.at[i], z, me)
-
-    interleave(n_b, n_a, make_b, make_a)
+        part(far_z)
+        push(own_a.at[far_z, low, :, :, cols], half_l.at[:, :, :, cols], zs, hl.at[i], right, me)
+        push(own_a.at[far_z, high, :, :, cols], half_r.at[:, :, :, cols], zs, hr.at[i], left, me)
+        each(3, lambda j: part(lax.rem(dp + 3 + j, ndp)))
+
+    def join(target, source, z, start, cols, n):
+        batch = min(4, n)
+        flat = (batch * cap, width)
+
+        def some(e):
+            here, there = pl.ds(start + e * batch, batch), pl.ds(e * batch, batch)
+            total = target[z, here, :, :, cols].reshape(flat).astype(F32)
+            total = total + source[there, :, :, cols].reshape(flat).astype(F32)
+            target[z, here, :, :, cols] = total.astype(BF).reshape(batch, cap // 2, 2, width)
+
+        each(n // batch, some)
+
+    def turn_a(i):
+        cols = span(i)
+        landed(half_l.at[:, :, :, cols], hl.at[i])
+        join(own_a, half_l, right, 0, cols, mid)
+        push(own_a.at[right, :, :, :, cols], from_l.at[:, :, :, cols], fs, fl.at[i], right, me)
+        landed(half_r.at[:, :, :, cols], hr.at[i])
+        join(own_a, half_r, left, mid, cols, mid)
+        push(own_a.at[left, :, :, :, cols], from_r.at[:, :, :, cols], fs, fr.at[i], left, me)
+
+    both = min(n_a, n_b)
+
+    def make(i):
+        make_a(i)
+        if_later(i, turn_a)
+        make_b(i)
+
+    def if_later(i, body):
+        @pl.when(i > 0)
+        def _():
+            body(i - 1)
+
+    each(both, make)
+
+    def make_more(i, carry):
+        if n_a > n_b:
+            make_a(i)
+            if_later(i, turn_a)
+        else:
+            make_b(i)
+        return carry
+
+    lax.fori_loop(both, max(n_a, n_b), make_more, 0)
 
     eye = jnp.where(
         lax.broadcasted_iota(jnp.int32, (tokens, tokens), 0)
@@ -487,21 +589,23 @@
 
     each(ndp, weigh)
 
+    if n_a:
+        turn_a(n_a - 1)
+
     def back_a(i):
         cols = span(i)
-        landed(from_z.at[pl.ds(0, ndp - 1), :, :, :, cols], zr.at[i])
-
-        def add(e, carry):
+        landed(from_l.at[:, :, :, cols], fl.at[i])
+        landed(from_r.at[:, :, :, cols], fr.at[i])
+
+        def add(e):
             some = pl.ds(e * 4, 4)
             flat = (4 * cap, width)
             total = own_a[dp, some, :, :, cols].reshape(flat).astype(F32)
-            for j in range(1, ndp):
-                z = lax.rem(dp + j, ndp)
-                total = total + from_z[z, some, :, :, cols].reshape(flat).astype(F32)
+            total = total + from_l[some, :, :, cols].reshape(flat).astype(F32)
+            total = total + from_r[some, :, :, cols].reshape(flat).astype(F32)
             send_a[some, :, :, cols] = total.astype(BF).reshape(4, cap // 2, 2, width)
-            return carry
-
-        lax.fori_loop(0, nseq // 4, add, 0)
+
+        each(nseq // 4, add)
         ret_a[me, :, :, cols] = send_a[me, :, :, cols]
 
         def go(d, carry):
@@ -543,7 +647,8 @@
 
     interleave(n_b, n_a, end_b, end_a)
     if n_a:
-        landed(own_a.at[pl.ds(0, ndp - 1)], zs)
+        landed(own_a.at[0], zs)
+        landed(own_a.at[pl.ds(0, 2)], fs)
         landed(send_a.at[pl.ds(0, nseq - 1)], as_)
     if n_b:
         landed(part_b.at[:, pl.ds(0, nseq - 1)], bs)
@@ -551,7 +656,7 @@
 
 
 def experts(
-    normed, base, q, k, v, g, run, factor, back, choice, slot, weights, w_in, w_out, ndp, nseq, cap, split
+    normed, base, q, k, v, g, run, factor, back, meta, w_in, w_out, ndp, nseq, cap, split
 ):
     tokens, model = normed.shape
     hidden = w_in.shape[1]
@@ -559,8 +664,6 @@
     rows = nseq * cap
     ca, cb = n_a * width, n_b * width
     cfg = (ndp, nseq, cap, width, n_a, n_b)
-    target = (choice * cap + slot).astype(F32).T
-    meta = jnp.concatenate([target, weights.T, jnp.zeros((4, tokens), F32)], axis=0)
     dma = pltpu.SemaphoreType.DMA
     whole = pl.BlockSpec(memory_space=pltpu.VMEM)
     away = pl.BlockSpec(memory_space=pl.ANY)
@@ -572,7 +675,7 @@
             jax.ShapeDtypeStruct((tokens, model), BF),
             jax.ShapeDtypeStruct((tokens, model), BF),
         ),
-        in_specs=[whole, whole, away] + [whole] * 7,
+        in_specs=[whole, whole] + [away] * 5 + [whole] * 3,
         out_specs=(whole,) * 4,
         scratch_shapes=[
             vmem(ndp, nseq, cap // 2, 2, model),
@@ -584,8 +687,13 @@
             vmem(hidden, model),
             vmem(ndp * rows, hidden, kind=F32),
             vmem(*back.shape),
-            dma, dma, dma, dma, dma((max(n_b, 1),)), dma, dma((max(n_a, 1),)),
-            dma, dma((max(n_b, 1),)), dma, dma((max(n_a, 1),)), dma, dma,
+            vmem(tokens, model),
+            vmem(tokens, model),
+            vmem(tokens, model),
+            vmem(tokens, model),
+            dma, dma((4,)), dma, dma, dma, dma((max(n_b, 1),)), dma, dma((max(n_a, 1),)),
+            dma, dma((max(n_b, 1),)), dma, dma((max(n_a, 1),)), dma((max(n_a, 1),)),
+            dma, dma((max(n_a, 1),)), dma((max(n_a, 1),)), dma, dma,
         ],
         compiler_params=pltpu.CompilerParams(
             collective_id=1, has_side_effects=True, vmem_limit_bytes=62 << 20
@@ -600,7 +708,10 @@
         scratch_shapes=[
             vmem(ndp, nseq, cap // 2, 2, max(ca, 128)),
             vmem(ndp, nseq, cap // 2, 2, max(cb, 128)),
-            vmem(ndp, nseq, cap // 2, 2, max(ca, 128)),
+            vmem(nseq // 2, cap // 2, 2, max(ca, 128)),
+            vmem(nseq // 2, cap // 2, 2, max(ca, 128)),
+            vmem(nseq, cap // 2, 2, max(ca, 128)),
+            vmem(nseq, cap // 2, 2, max(ca, 128)),
             vmem(nseq, cap // 2, 2, max(ca, 128)),
             vmem(nseq, cap // 2, 2, max(ca, 128)),
             vmem(ndp, nseq, cap // 2, 2, max(cb, 128)),
@@ -608,7 +719,8 @@
             vmem(ndp, tokens, max(cb, 128)),
             vmem(ndp, tokens, rows),
             vmem(hidden, model),
-            dma((n_a + n_b,)), dma, dma((max(n_a, 1),)), dma, dma((max(n_b, 1),)),
+            dma((n_a + n_b,)), dma, dma((max(n_a, 1),)), dma((max(n_a, 1),)),
+            dma, dma((max(n_a, 1),)), dma((max(n_a, 1),)), dma, dma((max(n_b, 1),)),
             dma, dma((max(n_a, 1),)), dma, dma((max(n_b, 1),)),
         ],
         compiler_params=pltpu.CompilerParams(
@@ -621,7 +733,7 @@
 
 norm_eps = 1e-06
 TOP = 2
-SPLIT = (4, 4, 512)
+SPLIT = (5, 3, 512)
 
 
 def on_device(
@@ -633,17 +745,15 @@
     heads = log_decay.shape[1]
     head = width // heads
     cap = max(2, TOP * length * 5 // (4 * nseq))
-    run = jnp.cumsum(log_decay[0], axis=1)
     factor = jnp.broadcast_to(jnp.exp2(grad_exponent.astype(F32))[:, None], (heads, head))
-    choice = route_ids[0]
-    flat = choice.reshape(length * TOP)
-    onehot = (flat[:, None] == jnp.arange(nseq, dtype=jnp.int32)[None, :]).astype(jnp.int32)
-    slot = jnp.sum((jnp.cumsum(onehot, axis=0) - 1) * onehot, axis=-1).reshape(length, TOP)
-    q, k, v, g = queries[0], keys[0], values[0], attn_grad[0]
-    attn_out, normed, back = attention(q, k, v, g, run, norm_gain[None], ndp, nseq, head)
+    args = (queries, keys, values, attn_grad)
+    ids = jnp.swapaxes(route_ids, 1, 2)
+    weights = jnp.swapaxes(route_weights, 1, 2)
+    attn_out, normed, back, run, meta = attention(
+        *args, log_decay, norm_gain[None], ids, weights, ndp, nseq, head, cap
+    )
     layer_out, key_out, value_out = experts(
-        normed, attn_out, q, k, v, g, run, factor, back, choice, slot, route_weights[0], w_in, w_out,
-        ndp, nseq, cap, SPLIT,
+        normed, attn_out, *args, run, factor, back, meta, w_in, w_out, ndp, nseq, cap, SPLIT
     )
     return (layer_out[None], key_out[None], value_out[None])
 

time: 274 us -> 239 us (0.87)
  Pallas kernels: 252 us -> 231 us
  local copies, waits for them, and re-layouts: 16.3 us -> 6.23 us
  other arithmetic: 4.44 us -> 0.66 us
    pallas_call x1, Pallas kernels: 96.2 us -> 84 us  [experts(): pl.pallas_call(functools.partial(combine_kernel, cfg), out_shape=jax.Shap...]
    pallas_call x1, Pallas kernels: 103 us -> 91 us  [experts(): pl.pallas_call(functools.partial(dispatch_kernel, cfg), out_shape=(jax.Sh...]
    unnamed x24 -> x5, local copies, waits for them, and re-layouts: 14.9 us -> 5.55 us
    pallas_call x1, Pallas kernels: 53.1 us -> 56.5 us  [attention(): pl.pallas_call(functools.partial(attention_kernel, (ndp, nseq, head, cap)...]
where the time goes in v2:
time: 239 us
  Pallas kernels  231 us (97%)
  local copies, waits for them, and re-layouts  6.23 us (3%)
    pallas_call x1, Pallas kernels, experts(): pl.pallas_call(functools.partial(dispatch_kernel, cfg), out_shape=(jax.Sh...  91 us
    pallas_call x1, Pallas kernels, experts(): pl.pallas_call(functools.partial(combine_kernel, cfg), out_shape=jax.Shap...  84 us
    pallas_call x1, Pallas kernels, attention(): pl.pallas_call(functools.partial(attention_kernel, (ndp, nseq, head, cap)...  56.5 us
    unnamed x5, local copies, waits for them, and re-layouts  5.55 us

profile of v2, /device:TPU:1, one launch (start us, length us, event | category | flops | bytes accessed | tf_op | source)
XLA Modules:
  0.0 239.0 jit_solution(3388862365634953474)
XLA Ops:
  0.6 0.7 multiply_exponential_fusion
  1.3 0.7 broadcast_in_dim.19.factor
  2.0 56.5 %attention.1 = (bf16[128,4096]{1,0:T(8,128)(2,1)}, bf16[128,4096]{1,0:T(8,128)(2,1)}, bf16[32,128,128]{2,1,0:T(8,128)(2,1)}, f32[32,128]{1,0:T(8,128)}, f32[8,128]{1,0:T(8,128)}) custom-call(bf16[1,128,4096]{2,1,0:T(8,128)(2,1)} %q_far.3, bf16[1,128,4096]{2,1,0:T(8,128)(2,1)} %k_far.3, bf16[1,128,4096]{2,1,0:T(8,128)(2,1)} %v_far.3, ...), custom_call_target="tpu_custom_call" | custom-call | tf_op jit(solution)/shard_map/attention/pallas_call | solution.py:271
  58.4 91.0 %dispatch.1 = (bf16[1280,1152]{1,0:T(8,128)(2,1)}, f32[4,8,128]{2,1,0:T(8,128)}, bf16[128,4096]{1,0:T(8,128)(2,1)}, bf16[128,4096]{1,0:T(8,128)(2,1)}) custom-call(bf16[128,4096]{1,0:T(8,128)(2,1)} %get-tuple-element.12.normed, f32[8,128]{1,0:T(8,128)} %get-tuple-element.13.meta, bf16[1,1152,4096]{2,1,0:T(8,128)(2,1)} %w_in.1, bf16[1,128,4096]{2,1,0:T(8,128)(2,1)} %q_far.3, ...), custom_call_target="tpu_custom_call" | custom-call | tf_op jit(solution)/shard_map/dispatch/pallas_call | solution.py:670
  149.5 0.0 copy-start
  149.5 84.0 %combine.1 = bf16[128,4096]{1,0:T(8,128)(2,1)} custom-call(bf16[1280,1152]{1,0:T(8,128)(2,1)} %get-tuple-element.16.hid, f32[4,8,128]{2,1,0:T(8,128)} %get-tuple-element.17.meta_all, bf16[1,1152,4096]{2,1,0:T(8,128)(2,1)} %w_out.1, bf16[128,4096]{1,0:T(8,128)(2,1)} %get-tuple-element.18.base), custom_call_target="tpu_custom_call" | custom-call | tf_op jit(solution)/shard_map/combine/pallas_call | solution.py:703
  233.5 2.3 copy.17
  235.8 2.3 copy.18
  238.0 0.0 copy-done
  238.1 1.0 copy.19
Async XLA Ops:
  149.5 88.6 %copy-start = (bf16[128,4096]{1,0:T(8,128)(2,1)S(1)}, bf16[128,4096]{1,0:T(8,128)(2,1)}, u32[]{:S(2)}) copy-start(bf16[128,4096]{1,0:T(8,128)(2,1)} %get-tuple-element.20) | copy-start | bytes 3145732
